TPU v7x, 32 devices: a whole 2x2x4 slice. The times are simulated.
32 devices in a mesh: shard: 4 (over y, x), replica: 8 (over z, core).
Axes of the slice: x: 2, y: 2, z: 4, core: 2. Of those that a mesh axis runs over, the one named last changes fastest.
Arguments:
- tokens: bfloat16 [8192, 1536], P(('shard', 'replica')), may hold values from -6 to 6
- cotangent: bfloat16 [8192, 1536], P(('shard', 'replica')), may hold values from -6 to 6
- seq_lengths: int32 [64], replicated, may hold values from 0 to 256, as said below
- seq_device: int32 [64], replicated, may hold values from 0 to 31
- seq_offsets: int32 [64], replicated, may hold values from 0 to 1
- norm_attn: bfloat16 [1, 1536], P(None, 'shard'), may hold values from 0.5 to 1.5
- w_qkv: bfloat16 [1, 1536, 3072], P(None, 'shard'), may hold values from -0.15625 to 0.15625
- w_out: bfloat16 [1, 1536, 1536], P(None, 'shard'), may hold values from -0.625 to 0.625
- norm_mlp: bfloat16 [1, 1536], P(None, 'shard'), may hold values from 0.5 to 1.5
- w_gate_up: bfloat16 [1, 1536, 8192], P(None, 'shard'), may hold values from -0.15625 to 0.15625
- w_down: bfloat16 [1, 4096, 1536], P(None, 'shard'), may hold values from -0.125 to 0.125
Outputs:
- result: bfloat16 [8192, 1536], P(('shard', 'replica'))
- grad_tokens: float32 [8192, 1536], P(('shard', 'replica'))
- grad_norm_attn: float32 [1, 1536], P(None, 'shard')
- grad_w_qkv: float32 [1, 1536, 3072], P(None, 'shard')
- grad_w_out: float32 [1, 1536, 1536], P(None, 'shard')
- grad_norm_mlp: float32 [1, 1536], P(None, 'shard')
- grad_w_gate_up: float32 [1, 1536, 8192], P(None, 'shard')
- grad_w_down: float32 [1, 4096, 1536], P(None, 'shard')
Inputs may be any that keep to these rules, and one draw needn't show every extreme that they name: `seq_lengths`: each device is named by exactly 2 entries. A sequence lies within blocks 2p and 2p + 1 of its device for some p; sequences of one device never share a row; length 0 marks an unused entry. In every draw some device is full, its every pair of blocks holding one sequence of length 256.
All inputs are finite; a program needn't handle non-finite values.
Results may differ from a plain program's by a relative error of at most 0.02.
Values may be sent and summed in bfloat16 or wider, within the bound.
A program may use at most 320 MiB of HBM per device.

v0:
```python
import jax
import jax.numpy as jnp
from jax import lax
from jax.sharding import PartitionSpec as P

HEADS = 16
KV_HEADS = 8
HEAD = 96
FF = 4096
BLOCK = 128
epsilon = 1e-05
rope_base = 100000.0


def rms_scale(field):
    return lax.rsqrt(jnp.mean(field * field, axis=-1, keepdims=True) + epsilon)


def rotate(field):
    half = field.shape[-1] // 2
    return jnp.concatenate([-field[..., half:], field[..., :half]], axis=-1)


def rope_tables(position):
    half = HEAD // 2
    freqs = rope_base ** (-(jnp.arange(half, dtype=jnp.float32) * 2.0) / HEAD)
    angles = position.astype(jnp.float32)[:, None] * freqs[None, :]
    cosine = jnp.cos(angles)
    sine = jnp.sin(angles)
    return (jnp.concatenate([cosine, cosine], axis=-1), jnp.concatenate([sine, sine], axis=-1))


def locate(device, seq_lengths, seq_device, seq_offsets, rows):
    starts = seq_offsets * BLOCK
    local = jnp.arange(rows, dtype=jnp.int32)
    labels = jnp.arange(seq_lengths.shape[0], dtype=jnp.int32)
    hits = (
        (seq_device[None, :] == device)
        & (local[:, None] >= starts[None, :])
        & (local[:, None] < (starts + seq_lengths)[None, :])
    )
    segment = jnp.max(jnp.where(hits, labels[None, :], -1), axis=1)
    begin = jnp.sum(jnp.where(hits, starts[None, :], 0), axis=1)
    return (segment, local - begin)


def mask_of(segment):
    local = jnp.arange(segment.shape[0], dtype=jnp.int32)
    return (segment[:, None] == segment[None, :]) & (local[None, :] <= local[:, None])


def contract_rows(left, right):
    return lax.dot_general(
        left, right, (((0,), (0,)), ((), ())), preferred_element_type=jnp.float32
    )


def contract_cols(left, right):
    return lax.dot_general(
        left, right, (((1,), (1,)), ((), ())), preferred_element_type=jnp.float32
    )


def norm_rows(field, gain):
    scale = rms_scale(field)
    normed = (field * scale * gain.astype(jnp.float32)[None, :]).astype(jnp.bfloat16)
    return (scale, normed)


def norm_back(grad_normed, field, scale, gain):
    normed = field * scale
    grad_gain = jnp.sum(grad_normed * normed, axis=0)
    inner = grad_normed * gain[None, :]
    grad_field = scale * (inner - normed * jnp.mean(inner * normed, axis=-1, keepdims=True))
    return (grad_field, grad_gain)


def split_project(project, q_heads, k_heads, cosine, sine):
    rows = project.shape[0]
    width_q = q_heads * HEAD
    width_k = k_heads * HEAD
    queries = project[:, :width_q].reshape(rows, q_heads, HEAD)
    keys = project[:, width_q : width_q + width_k].reshape(rows, k_heads, HEAD)
    values_b = project[:, width_q + width_k :].reshape(rows, k_heads, HEAD).astype(jnp.bfloat16)
    queries_b = (queries * cosine[:, None, :] + rotate(queries) * sine[:, None, :]).astype(
        jnp.bfloat16
    )
    keys_b = (keys * cosine[:, None, :] + rotate(keys) * sine[:, None, :]).astype(jnp.bfloat16)
    return (queries_b, keys_b, values_b)


def join_grads(grad_queries, grad_keys, grad_values, cosine, sine):
    rows = grad_queries.shape[0]
    grad_queries = grad_queries * cosine[:, None, :] - rotate(grad_queries * sine[:, None, :])
    grad_keys = grad_keys * cosine[:, None, :] - rotate(grad_keys * sine[:, None, :])
    return jnp.concatenate(
        [
            grad_queries.reshape(rows, -1),
            grad_keys.reshape(rows, -1),
            grad_values.reshape(rows, -1),
        ],
        axis=1,
    ).astype(jnp.bfloat16)


def attention_scores(queries_b, keys_b, allowed):
    rows = queries_b.shape[0]
    kv_count = keys_b.shape[1]
    grouped = queries_b.reshape(rows, kv_count, queries_b.shape[1] // kv_count, HEAD)
    scores = jnp.einsum(
        "qkgd,pkd->kgqp", grouped, keys_b, preferred_element_type=jnp.float32
    ) * HEAD ** (-0.5)
    return jnp.where(allowed, scores, -1e30)


def attend_forward(queries_b, keys_b, values_b, allowed):
    rows = queries_b.shape[0]
    scores = attention_scores(queries_b, keys_b, allowed)
    top = jnp.max(scores, axis=-1, keepdims=True)
    total = jnp.log(jnp.sum(jnp.exp(scores - top), axis=-1, keepdims=True)) + top
    weights_b = jnp.exp(scores - total).astype(jnp.bfloat16)
    mixed = jnp.einsum("kgqp,pkd->qkgd", weights_b, values_b, preferred_element_type=jnp.float32)
    return (mixed.reshape(rows, -1).astype(jnp.bfloat16), total)


def attend_backward(grad_mixed_b, queries_b, keys_b, values_b, total, allowed):
    rows = queries_b.shape[0]
    q_heads = queries_b.shape[1]
    kv_count = keys_b.shape[1]
    per = q_heads // kv_count
    factor = HEAD ** (-0.5)
    grad_mixed = grad_mixed_b.reshape(rows, kv_count, per, HEAD)
    weights = jnp.exp(attention_scores(queries_b, keys_b, allowed) - total)
    weights_b = weights.astype(jnp.bfloat16)
    grad_values = jnp.einsum(
        "kgqp,qkgd->pkd", weights_b, grad_mixed, preferred_element_type=jnp.float32
    )
    grad_weights = jnp.einsum(
        "qkgd,pkd->kgqp", grad_mixed, values_b, preferred_element_type=jnp.float32
    )
    grad_scores = weights * (grad_weights - jnp.sum(weights * grad_weights, axis=-1, keepdims=True))
    grad_scores_b = grad_scores.astype(jnp.bfloat16)
    grouped = queries_b.reshape(rows, kv_count, per, HEAD)
    grad_queries = jnp.einsum(
        "kgqp,pkd->qkgd", grad_scores_b, keys_b, preferred_element_type=jnp.float32
    )
    grad_queries = grad_queries.reshape(rows, q_heads, HEAD) * factor
    grad_keys = (
        jnp.einsum("kgqp,qkgd->pkd", grad_scores_b, grouped, preferred_element_type=jnp.float32)
        * factor
    )
    return (grad_queries, grad_keys, grad_values)


def gate_back(grad_hidden, gate_up, local_ff):
    gate = gate_up[:, :local_ff]
    upper = gate_up[:, local_ff:]
    sigma = jax.nn.sigmoid(gate)
    grad_gate = grad_hidden * upper * sigma * (1.0 + gate * (1.0 - sigma))
    grad_upper = grad_hidden * (gate * sigma)
    return jnp.concatenate([grad_gate, grad_upper], axis=1).astype(jnp.bfloat16)


def attention_forward(field, gain, w_project, w_output, allowed, cosine, sine):
    scale, normed = norm_rows(field, gain)
    project = jnp.dot(normed, w_project, preferred_element_type=jnp.float32)
    queries_b, keys_b, values_b = split_project(project, HEADS, KV_HEADS, cosine, sine)
    mixed, total = attend_forward(queries_b, keys_b, values_b, allowed)
    after = field + jnp.dot(mixed, w_output, preferred_element_type=jnp.float32)
    return (after, (scale, normed, queries_b, keys_b, values_b, total, mixed))


def attention_backward(grad_field, field, gain, w_project, w_output, saved, allowed, cosine, sine):
    scale, normed, queries_b, keys_b, values_b, total, mixed = saved
    grad_branch = grad_field.astype(jnp.bfloat16)
    grad_w_output = contract_rows(mixed, grad_branch)
    grad_mixed = contract_cols(grad_branch, w_output).astype(jnp.bfloat16)
    grad_queries, grad_keys, grad_values = attend_backward(
        grad_mixed, queries_b, keys_b, values_b, total, allowed
    )
    grad_project = join_grads(grad_queries, grad_keys, grad_values, cosine, sine)
    grad_w_project = contract_rows(normed, grad_project)
    grad_normed = contract_cols(grad_project, w_project)
    grad_input, grad_gain = norm_back(grad_normed, field, scale, gain.astype(jnp.float32))
    return (grad_field + grad_input, grad_gain, grad_w_project, grad_w_output)


def mlp_forward(field, gain, w_gateup, w_lower):
    scale, normed = norm_rows(field, gain)
    gate_up = jnp.dot(normed, w_gateup, preferred_element_type=jnp.float32)
    hidden = (jax.nn.silu(gate_up[:, :FF]) * gate_up[:, FF:]).astype(jnp.bfloat16)
    after = field + jnp.dot(hidden, w_lower, preferred_element_type=jnp.float32)
    return (after, (scale, normed, gate_up, hidden))


def mlp_backward(grad_field, field, gain, w_gateup, w_lower, saved):
    scale, normed, gate_up, hidden = saved
    grad_branch = grad_field.astype(jnp.bfloat16)
    grad_w_lower = contract_rows(hidden, grad_branch)
    grad_hidden = contract_cols(grad_branch, w_lower)
    grad_gateup = gate_back(grad_hidden, gate_up, FF)
    grad_w_gateup = contract_rows(normed, grad_gateup)
    grad_normed = contract_cols(grad_gateup, w_gateup)
    grad_input, grad_gain = norm_back(grad_normed, field, scale, gain.astype(jnp.float32))
    return (grad_field + grad_input, grad_gain, grad_w_gateup, grad_w_lower)


def settle(owned):
    return (
        lax.psum(owned[0].astype(jnp.bfloat16), "replica").astype(jnp.float32),
        lax.psum(owned[1].astype(jnp.bfloat16), "replica").astype(jnp.float32),
        lax.psum(owned[2].astype(jnp.bfloat16), "replica").astype(jnp.float32),
        lax.psum(owned[3].astype(jnp.bfloat16), "replica").astype(jnp.float32),
        lax.psum(owned[4].astype(jnp.bfloat16), "replica").astype(jnp.float32),
        lax.psum(owned[5].astype(jnp.bfloat16), "replica").astype(jnp.float32),
    )


def body(
    tokens,
    cotangent,
    seq_lengths,
    seq_device,
    seq_offsets,
    norm_attn,
    w_qkv,
    w_out,
    norm_mlp,
    w_gate_up,
    w_down,
):
    rows = tokens.shape[0]
    layers = w_qkv.shape[0]
    device = lax.axis_index(("shard", "replica"))
    segment, position = locate(device, seq_lengths, seq_device, seq_offsets, rows)
    live = (segment >= 0).astype(jnp.float32)[:, None]
    field = tokens.astype(jnp.float32)
    per_layer = [None] * layers
    cosine, sine = rope_tables(position)
    allowed = mask_of(segment)
    layer = 0
    attn_parts = (
        lax.all_gather(norm_attn[layer], "shard", axis=0, tiled=True),
        lax.all_gather(w_qkv[layer], "shard", axis=0, tiled=True),
        lax.all_gather(w_out[layer], "shard", axis=0, tiled=True),
    )
    middle, attn_saved = attention_forward(
        field, attn_parts[0], attn_parts[1], attn_parts[2], allowed, cosine, sine
    )
    mlp_parts = (
        lax.all_gather(norm_mlp[layer], "shard", axis=0, tiled=True),
        lax.all_gather(w_gate_up[layer], "shard", axis=0, tiled=True),
        lax.all_gather(w_down[layer], "shard", axis=0, tiled=True),
    )
    after, mlp_saved = mlp_forward(middle, mlp_parts[0], mlp_parts[1], mlp_parts[2])
    kept_inputs = [(field, attn_saved, middle, mlp_saved)]
    result = (after * live).astype(jnp.bfloat16)
    grad_field = cotangent.astype(jnp.float32) * live
    for layer in reversed(range(layers)):
        field_in, attn_saved, middle, mlp_saved = kept_inputs[layer]
        mlp_parts = (
            lax.all_gather(norm_mlp[layer], "shard", axis=0, tiled=True),
            lax.all_gather(w_gate_up[layer], "shard", axis=0, tiled=True),
            lax.all_gather(w_down[layer], "shard", axis=0, tiled=True),
        )
        grad_middle, grad_gain_mlp, grad_gateup, grad_lower = mlp_backward(
            grad_field, middle, mlp_parts[0], mlp_parts[1], mlp_parts[2], mlp_saved
        )
        mlp_owned = (
            lax.psum_scatter(
                grad_gain_mlp.astype(jnp.bfloat16), "shard", scatter_dimension=0, tiled=True
            ).astype(jnp.float32),
            lax.psum_scatter(
                grad_gateup.astype(jnp.bfloat16), "shard", scatter_dimension=0, tiled=True
            ).astype(jnp.float32),
            lax.psum_scatter(
                grad_lower.astype(jnp.bfloat16), "shard", scatter_dimension=0, tiled=True
            ).astype(jnp.float32),
        )
        attn_parts = (
            lax.all_gather(norm_attn[layer], "shard", axis=0, tiled=True),
            lax.all_gather(w_qkv[layer], "shard", axis=0, tiled=True),
            lax.all_gather(w_out[layer], "shard", axis=0, tiled=True),
        )
        grad_field, grad_gain_attn, grad_project, grad_output = attention_backward(
            grad_middle,
            field_in,
            attn_parts[0],
            attn_parts[1],
            attn_parts[2],
            attn_saved,
            allowed,
            cosine,
            sine,
        )
        attn_owned = (
            lax.psum_scatter(
                grad_gain_attn.astype(jnp.bfloat16), "shard", scatter_dimension=0, tiled=True
            ).astype(jnp.float32),
            lax.psum_scatter(
                grad_project.astype(jnp.bfloat16), "shard", scatter_dimension=0, tiled=True
            ).astype(jnp.float32),
            lax.psum_scatter(
                grad_output.astype(jnp.bfloat16), "shard", scatter_dimension=0, tiled=True
            ).astype(jnp.float32),
        )
        per_layer[layer] = settle(
            (attn_owned[0], attn_owned[1], attn_owned[2], mlp_owned[0], mlp_owned[1], mlp_owned[2])
        )
    stacked = [jnp.stack([entry[member] for entry in per_layer], axis=0) for member in range(6)]
    return (
        result,
        grad_field,
        stacked[0],
        stacked[1],
        stacked[2],
        stacked[3],
        stacked[4],
        stacked[5],
    )


def solution(mesh):
    placed = (
        P(("shard", "replica"), None),
        P(("shard", "replica"), None),
        P(),
        P(),
        P(),
        P(None, "shard"),
        P(None, "shard", None),
        P(None, "shard", None),
        P(None, "shard"),
        P(None, "shard", None),
        P(None, "shard", None),
    )
    return jax.shard_map(
        body,
        mesh=mesh,
        in_specs=placed,
        out_specs=(
            P(("shard", "replica"), None),
            P(("shard", "replica"), None),
            P(None, "shard"),
            P(None, "shard", None),
            P(None, "shard", None),
            P(None, "shard"),
            P(None, "shard", None),
            P(None, "shard", None),
        ),
        check_vma=False,
    )
```

profile of v0, /device:TPU:0, one launch (start us, length us, event | category | flops | bytes accessed | tf_op | source)
XLA Modules:
  0.0 1345.5 jit_solution(480248952729375393)
XLA Ops:
  10.1 9.6 all-gather
  19.7 8.2 all-gather.3
  30.7 78.1 %all-gather.11.cloned.1.call-done = bf16[1,1536,3072]{2,1,0:T(8,128)(2,1)} async-done(((bf16[1,384,3072]{2,1,0:T(8,128)(2,1)}), bf16[1,1536,3072]{2,1,0:T(8,128)(2,1)}) %all-gather.11.cloned.1.call-update) | async-done | bytes 9437200 | tf_op jit(solution)/shard_map/all_gather | solution.py:244
  108.8 5.2 fusion.10
  125.3 42.3 %all-gather.13.cloned.1.call-done = bf16[1,1536,1536]{2,1,0:T(8,128)(2,1)} async-done(((bf16[1,384,1536]{2,1,0:T(8,128)(2,1)}), bf16[1,1536,1536]{2,1,0:T(8,128)(2,1)}) %all-gather.13.cloned.1.call-update) | async-done | bytes 4718608 | tf_op jit(solution)/shard_map/all_gather | solution.py:245
  167.6 3.8 multiply_reduce_fusion.2
  171.4 225.6 %all-gather.15.cloned.1.call-done = bf16[1,1536,8192]{2,1,0:T(8,128)(2,1)} async-done(((bf16[1,384,8192]{2,1,0:T(8,128)(2,1)}), bf16[1,1536,8192]{2,1,0:T(8,128)(2,1)}) %all-gather.15.cloned.1.call-update) | async-done | bytes 25165840 | tf_op jit(solution)/shard_map/all_gather | solution.py:252
  397.1 13.8 %fusion.2 = f32[256,8192]{1,0:T(8,128)} fusion(bf16[1,1536,8192]{2,1,0:T(8,128)(2,1)} %all-gather.15.cloned.1.call-done, f32[256,1536]{1,0:T(8,128)S(1)} %get-tuple-element.44, f32[1536]{0:T(1024)S(1)} %convert_reduce_fusion, f32[256]{0:T(256)S(1)} %add_rsqrt_fusion), kind=kOutput, calls=%fused_computation.3 | convolution fusion | flops 6443630592 | bytes 35134464 | tf_op jit(solution)/shard_map/dot_general | solution.py:190
  410.9 110.3 %all-gather.17.cloned.1.call-done = bf16[1,4096,1536]{2,1,0:T(8,128)(2,1)} async-done(((bf16[1,1024,1536]{2,1,0:T(8,128)(2,1)}), bf16[1,4096,1536]{2,1,0:T(8,128)(2,1)}) %all-gather.17.cloned.1.call-update) | async-done | bytes 12582928 | tf_op jit(solution)/shard_map/all_gather | solution.py:253
  521.2 10.4 multiply_convert_fusion.1
  531.6 14.9 %multiply_reduce_fusion = (bf16[1536]{0:T(1024)(128)(2,1)}, f32[256]{0:T(256)S(1)}, f32[256,1536]{1,0:T(8,128)}) fusion(f32[256,1536]{1,0:T(8,128)S(1)} %get-tuple-element.44, f32[256]{0:T(256)S(1)} %add_rsqrt_fusion, f32[1536]{0:T(1024)S(1)} %convert_reduce_fusion, bf16[1,1536,8192]{2,1,0:T(8,128)(2,1)} %all-gather.15.cloned.1.call-done, ...), kind=kOutput, calls=%fused_computation.63 | convolution fusion | flops 6453196800 | bytes 32517120 | tf_op jit(solution)/shard_map/dot_general | solution.py:59
  548.5 3.6 convolution_convert_fusion.3
  552.2 4.6 fusion.33
  556.8 2.3 copy.56
  559.1 4.2 fusion.16
  570.9 7.3 convolution_convert_fusion.2
  578.3 10.2 convolution_convert_fusion.1
  588.5 14.2 %convolution_convert_fusion = bf16[1536,8192]{1,0:T(8,128)(2,1)} fusion(bf16[256,4096]{1,0:T(8,128)(2,1)} %copy-done.16, bf16[256,4096]{1,0:T(8,128)(2,1)} %copy-done.15, f32[256,1536]{1,0:T(8,128)S(1)} %get-tuple-element.44, f32[1536]{0:T(1024)S(1)} %convert_reduce_fusion, f32[256]{0:T(256)} %copy-done.27), kind=kOutput, calls=%fused_computation | convolution fusion | flops 6464602112 | bytes 30940160 | tf_op jit(solution)/shard_map/dot_general | solution.py:53
  603.0 6.2 reduce-scatter.7.cloned.1.call-done
  609.2 97.9 %reduce-scatter.5.cloned.1.call-done = bf16[384,3072]{1,0:T(8,128)(2,1)} async-done(((bf16[1536,3072]{1,0:T(8,128)(2,1)}), bf16[384,3072]{1,0:T(8,128)(2,1)}) %reduce-scatter.5.cloned.1.call-update) | async-done | bytes 2359312 | tf_op jit(solution)/shard_map/reduce_scatter | solution.py:300
  707.1 124.3 %reduce-scatter.11.cloned.1.call-done = bf16[1024,1536]{1,0:T(8,128)(2,1)} async-done(((bf16[4096,1536]{1,0:T(8,128)(2,1)}), bf16[1024,1536]{1,0:T(8,128)(2,1)}) %reduce-scatter.11.cloned.1.call-update) | async-done | bytes 3145744 | tf_op jit(solution)/shard_map/reduce_scatter | solution.py:276
  831.4 224.9 %reduce-scatter.9.cloned.1.call-done = bf16[384,8192]{1,0:T(8,128)(2,1)} async-done(((bf16[1536,8192]{1,0:T(8,128)(2,1)}), bf16[384,8192]{1,0:T(8,128)(2,1)}) %reduce-scatter.9.cloned.1.call-update) | async-done | bytes 6291472 | tf_op jit(solution)/shard_map/reduce_scatter | solution.py:273
  1058.2 8.8 fusion.46
  1067.0 9.2 all-reduce.4
  1076.4 15.4 %all-reduce.2 = (bf16[1,384]{1,0:T(2,128)(2,1)S(1)}, bf16[1,384]{1,0:T(2,128)(2,1)S(1)}) all-reduce(bf16[1,384]{1,0:T(2,128)(2,1)S(1)} %stack.36, bf16[1,384]{1,0:T(2,128)(2,1)S(1)} %stack.42), channel_id=1, replica_groups=mesh['shard'=4,'replica'=8] {'replica'}, use_global_device_ids=true, to_apply=%region_11.12 | all-reduce | flops 768 | bytes 3072 | tf_op jit(solution)/shard_map/psum | solution.py:210
  1093.6 3.4 fusion.45
  1096.9 9.0 fusion.30
  1105.9 215.4 %all-reduce.7.cloned.1.call-done = (bf16[1,384,3072]{2,1,0:T(8,128)(2,1)}, bf16[1,384,1536]{2,1,0:T(8,128)(2,1)}, bf16[1,384,8192]{2,1,0:T(8,128)(2,1)}, bf16[1,1024,1536]{2,1,0:T(8,128)(2,1)}) async-done(((bf16[1,384,3072]{2,1,0:T(8,128)(2,1)}, bf16[1,384,1536]{2,1,0:T(8,128)(2,1)}, bf16[1,384,8192]{2,1,0:T(8,128)(2,1)}, bf16[1,1024,1536]{2,1,0:T(8,128)(2,1)}), (bf16[1,384,3072]{2,1,0:T(8,128)(2,1)}, ...) | async-done | bytes 12976144 | tf_op jit(solution)/shard_map/psum | solution.py:211
  1321.3 4.6 stack.39
  1325.9 3.0 stack.41
  1328.8 6.3 stack.45
  1335.2 3.6 stack.47
  (148 shorter events, 29.8 us)
Async XLA Ops:
  7.2 101.6 %all-gather.11.cloned.1.call-start = ((), (), s32[]{:S(2)}) async-start(), calls=%async_computation.8 | async-start | bytes 11796480 | tf_op jit(solution)/shard_map/all_gather | solution.py:244
  7.9 159.7 %all-gather.13.cloned.1.call-start = ((), (), s32[]{:S(2)}) async-start(), calls=%async_computation.9 | async-start | bytes 5898240 | tf_op jit(solution)/shard_map/all_gather | solution.py:245
  8.7 388.4 %all-gather.15.cloned.1.call-start = ((), (), s32[]{:S(2)}) async-start(), calls=%async_computation.10 | async-start | bytes 31457280 | tf_op jit(solution)/shard_map/all_gather | solution.py:252
  9.4 10.3 copy-start.36
  9.4 18.5 %copy-start.39 = (s32[64]{0:T(128)S(1)}, s32[64]{0:T(128)}, u32[]{:S(2)}) copy-start(s32[64]{0:T(128)} %param.14) | copy-start | bytes 772
  9.4 18.6 %copy-start.37 = (s32[64]{0:T(128)S(1)}, s32[64]{0:T(128)}, u32[]{:S(2)}) copy-start(s32[64]{0:T(128)} %param.15) | copy-start | bytes 772
  9.4 18.6 %copy-start.38 = (s32[64]{0:T(128)S(1)}, s32[64]{0:T(128)}, u32[]{:S(2)}) copy-start(s32[64]{0:T(128)} %param.13) | copy-start | bytes 772
  9.4 19.7 %copy-start.2 = (bf16[256,1536]{1,0:T(8,128)(2,1)S(1)}, bf16[256,1536]{1,0:T(8,128)(2,1)}, u32[]{:S(2)}) copy-start(bf16[256,1536]{1,0:T(8,128)(2,1)} %param.11) | copy-start | bytes 2359300
  9.4 511.8 %all-gather.17.cloned.1.call-start = ((), (), s32[]{:S(2)}) async-start(), calls=%async_computation.11 | async-start | bytes 15728640 | tf_op jit(solution)/shard_map/all_gather | solution.py:253
  10.0 599.2 %reduce-scatter.7.cloned.1.call-start = ((), (), s32[]{:S(2)}) async-start(), calls=%async_computation.5 | async-start | bytes 5898240 | tf_op jit(solution)/shard_map/reduce_scatter | solution.py:303
  29.4 84.6 %copy-start.28 = (f32[256]{0:T(256)}, f32[256]{0:T(256)S(1)}, u32[]{:S(2)}) copy-start(f32[256]{0:T(256)S(1)} %add_rsqrt_fusion.1) | copy-start | bytes 3076
  125.3 46.1 %copy-start.4 = (bf16[8,96,2,256]{3,1,2,0:T(8,128)(2,1)}, bf16[8,96,2,256]{3,1,2,0:T(8,128)(2,1)S(1)}, u32[]{:S(2)}) copy-start(bf16[8,96,2,256]{3,1,2,0:T(8,128)(2,1)S(1)} %convolution_convert_fusion.4) | copy-start | bytes 2359300
  171.4 360.2 %copy-start.27 = (f32[256]{0:T(256)}, f32[256]{0:T(256)S(1)}, u32[]{:S(2)}) copy-start(f32[256]{0:T(256)S(1)} %add_rsqrt_fusion) | copy-start | bytes 3076
  397.1 124.1 %copy-start.10 = (bf16[256,1536]{1,0:T(8,128)(2,1)S(1)}, bf16[256,1536]{1,0:T(8,128)(2,1)}, u32[]{:S(2)}) copy-start(bf16[256,1536]{1,0:T(8,128)(2,1)} %param.12) | copy-start | bytes 2359300
  397.1 124.1 %copy-start.31 = (f32[256]{0:T(256)S(1)}, f32[256]{0:T(256)}, u32[]{:S(2)}) copy-start(f32[256]{0:T(256)} %compare_convert_fusion) | copy-start | bytes 3076
  531.6 14.9 %copy-start.15 = (bf16[256,4096]{1,0:T(8,128)(2,1)}, bf16[256,4096]{1,0:T(8,128)(2,1)S(1)}, u32[]{:S(2)}) copy-start(bf16[256,4096]{1,0:T(8,128)(2,1)S(1)} %get-tuple-element.22) | copy-start | bytes 6291460
  531.6 14.9 %copy-start.16 = (bf16[256,4096]{1,0:T(8,128)(2,1)}, bf16[256,4096]{1,0:T(8,128)(2,1)S(1)}, u32[]{:S(2)}) copy-start(bf16[256,4096]{1,0:T(8,128)(2,1)S(1)} %get-tuple-element.23) | copy-start | bytes 6291460
  531.6 14.9 %copy-start.11 = (bf16[256,1536]{1,0:T(8,128)(2,1)S(1)}, bf16[256,1536]{1,0:T(8,128)(2,1)}, u32[]{:S(2)}) copy-start(bf16[256,1536]{1,0:T(8,128)(2,1)} %param.12) | copy-start | bytes 2359300
  531.6 14.9 %copy-start.32 = (f32[256]{0:T(256)S(1)}, f32[256]{0:T(256)}, u32[]{:S(2)}) copy-start(f32[256]{0:T(256)} %compare_convert_fusion) | copy-start | bytes 3076
  552.1 155.0 %reduce-scatter.5.cloned.1.call-start = ((), (), s32[]{:S(2)}) async-start(), calls=%async_computation.4 | async-start | bytes 11796480 | tf_op jit(solution)/shard_map/reduce_scatter | solution.py:300
  559.1 4.2 copy-start.1
  559.1 4.2 copy-start.18
  559.1 4.2 copy-start.26
  567.0 3.1 copy-start.14
  578.2 253.2 %reduce-scatter.11.cloned.1.call-start = ((), (), s32[]{:S(2)}) async-start(), calls=%async_computation.7 | async-start | bytes 15728640 | tf_op jit(solution)/shard_map/reduce_scatter | solution.py:276
  588.5 467.8 %reduce-scatter.9.cloned.1.call-start = ((), (), s32[]{:S(2)}) async-start(), calls=%async_computation.6 | async-start | bytes 31457280 | tf_op jit(solution)/shard_map/reduce_scatter | solution.py:273
  602.8 718.6 %all-reduce.7.cloned.1.call-start = ((), (), s32[]{:S(2)}) async-start(), calls=%async_computation.12 | async-start | bytes 25952256 | tf_op jit(solution)/shard_map/psum | solution.py:211
  1058.2 8.8 copy-start.34
  1093.6 3.4 copy-start.9
  1093.6 3.4 copy-start.33
  1321.3 7.5 copy-start.8
  1328.8 6.3 copy-start.13
  (18 other events, 24.2 us)
Sparse Core Ops, SparseCore 0:
  9.8 98.9 all-gather.10
  110.6 56.9 all-gather.12
  169.5 227.5 all-gather.14
  398.8 122.4 all-gather.16
  552.3 56.9 reduce-scatter.6
  612.2 94.8 reduce-scatter.4
  710.8 120.5 reduce-scatter.10
  834.5 221.7 reduce-scatter.8
  1058.9 262.3 all-reduce.6
where the time goes:
time: 1350 us
  waiting for transfers between devices  1130 us (84%)
  matrix products  114 us (8%)
  blocking collectives  42.4 us (3%)
  other arithmetic  32 us (2%)
  between operations  15.3 us (1%)
    all_gather x1, waiting for transfers between devices, body(): lax.all_gather(w_gate_up[layer], 'shard', axis=0, tiled=True)  226 us
    reduce_scatter x1, waiting for transfers between devices, body(): lax.psum_scatter(grad_gateup.astype(jnp.bfloat16), 'shard', scatter_dimen...  225 us
    psum x1, waiting for transfers between devices, settle(): lax.psum(owned[1].astype(jnp.bfloat16), 'replica').astype(jnp.float32)  215 us
    reduce_scatter x1, waiting for transfers between devices, body(): lax.psum_scatter(grad_lower.astype(jnp.bfloat16), 'shard', scatter_dimens...  124 us
    all_gather x1, waiting for transfers between devices, body(): lax.all_gather(w_down[layer], 'shard', axis=0, tiled=True)  110 us
    reduce_scatter x1, waiting for transfers between devices, body(): lax.psum_scatter(grad_project.astype(jnp.bfloat16), 'shard', scatter_dime...  97.9 us
    all_gather x1, waiting for transfers between devices, body(): lax.all_gather(w_qkv[layer], 'shard', axis=0, tiled=True)  78.1 us
    all_gather x1, waiting for transfers between devices, body(): lax.all_gather(w_out[layer], 'shard', axis=0, tiled=True)  42.3 us
  transfers between devices with their start and end apart: 9, of which 9 were waited for; matrix products, arithmetic and copies ran while one was open for 8% of the time, Pallas kernels for 0%

commit v1 on v0

--- a/solution.py
+++ b/solution.py
@@ -10,6 +10,30 @@
 BLOCK = 128
 epsilon = 1e-05
 rope_base = 100000.0
+
+
+def part_loops(inp):
+    inter = lax.psum(1, "shard")
+    r_now = lax.axis_index("shard")
+    reached, y1, k_now = (inter, r_now, inp.shape[0])
+    p_next = jnp.zeros(
+        [dd * reached if s == 0 else dd for s, dd in enumerate(inp.shape)], inp.dtype
+    )
+    val2 = right_arr = inp
+    value_now = lax.dynamic_update_slice_in_dim(p_next, inp, y1 * k_now, axis=0)
+    for w in range(1, reached // 2 + 1):
+        val2 = lax.ppermute(val2, "shard", [(s, (s + 1) % reached) for s in range(reached)])
+        value_now = lax.dynamic_update_slice_in_dim(
+            value_now, val2, (y1 - w) % reached * k_now, axis=0
+        )
+        if 2 * w < reached:
+            right_arr = lax.ppermute(
+                right_arr, "shard", [(s, (s - 1) % reached) for s in range(reached)]
+            )
+            value_now = lax.dynamic_update_slice_in_dim(
+                value_now, right_arr, (y1 + w) % reached * k_now, axis=0
+            )
+    return value_now
 
 
 def rms_scale(field):
@@ -250,7 +274,7 @@
     mlp_parts = (
         lax.all_gather(norm_mlp[layer], "shard", axis=0, tiled=True),
         lax.all_gather(w_gate_up[layer], "shard", axis=0, tiled=True),
-        lax.all_gather(w_down[layer], "shard", axis=0, tiled=True),
+        part_loops(w_down[layer]),
     )
     after, mlp_saved = mlp_forward(middle, mlp_parts[0], mlp_parts[1], mlp_parts[2])
     kept_inputs = [(field, attn_saved, middle, mlp_saved)]

time: 1350 us -> 1460 us (1.081)
  waiting for transfers between devices: 1130 us -> 1220 us
  local copies, waits for them, and re-layouts: 13.2 us -> 33.7 us
    reduce_scatter x1, waiting for transfers between devices: 97.9 us -> 175 us  [body(): lax.psum_scatter(grad_project.astype(jnp.bfloat16), 'shard', scatter_dime...]
    psum x1, waiting for transfers between devices: 215 us -> 148 us  [settle(): lax.psum(owned[1].astype(jnp.bfloat16), 'replica').astype(jnp.float32)]
    ppermute x0 -> x3, waiting for transfers between devices: none -> 51.8 us  [the longest x2 51.8 us: part_loops(): lax.ppermute(val2, 'shard', [(s, (s + 1) % reached) for s in range(reache...]
    reduce_scatter x1, waiting for transfers between devices: 124 us -> 156 us  [body(): lax.psum_scatter(grad_lower.astype(jnp.bfloat16), 'shard', scatter_dimens...]
  transfers between devices with their start and end apart: 9 -> 12, of which waited for: 9 -> 10; matrix products, arithmetic and copies ran while one was open for 8% -> 9% of each run, Pallas kernels for 0% -> 0%
where the time goes in v1:
time: 1460 us
  waiting for transfers between devices  1220 us (84%)
  matrix products  110 us (8%)
  blocking collectives  40.7 us (3%)
  local copies, waits for them, and re-layouts  33.7 us (2%)
  other arithmetic  31.9 us (2%)
  between operations  15.3 us (1%)
    all_gather x1, waiting for transfers between devices, body(): lax.all_gather(w_gate_up[layer], 'shard', axis=0, tiled=True)  226 us
    reduce_scatter x1, waiting for transfers between devices, body(): lax.psum_scatter(grad_gateup.astype(jnp.bfloat16), 'shard', scatter_dimen...  225 us
    reduce_scatter x1, waiting for transfers between devices, body(): lax.psum_scatter(grad_project.astype(jnp.bfloat16), 'shard', scatter_dime...  175 us
    reduce_scatter x1, waiting for transfers between devices, body(): lax.psum_scatter(grad_lower.astype(jnp.bfloat16), 'shard', scatter_dimens...  156 us
    psum x1, waiting for transfers between devices, settle(): lax.psum(owned[1].astype(jnp.bfloat16), 'replica').astype(jnp.float32)  148 us
    all_gather x1, waiting for transfers between devices, body(): lax.all_gather(w_down[layer], 'shard', axis=0, tiled=True)  110 us
    all_gather x1, waiting for transfers between devices, body(): lax.all_gather(w_qkv[layer], 'shard', axis=0, tiled=True)  78.1 us
    ppermute x2, waiting for transfers between devices, part_loops(): lax.ppermute(val2, 'shard', [(s, (s + 1) % reached) for s in range(reache...  51.8 us
  transfers between devices with their start and end apart: 12, of which 10 were waited for; matrix products, arithmetic and copies ran while one was open for 9% of the time, Pallas kernels for 0%

profile of v1, /device:TPU:0, one launch (start us, length us, event | category | flops | bytes accessed | tf_op | source)
XLA Modules:
  0.0 1455.3 jit_solution(10181029838207990703)
XLA Ops:
  10.1 9.6 all-gather
  19.7 8.2 all-gather.3
  30.7 78.1 %all-gather.11.cloned.1.call-done = bf16[1,1536,3072]{2,1,0:T(8,128)(2,1)} async-done(((bf16[1,384,3072]{2,1,0:T(8,128)(2,1)}), bf16[1,1536,3072]{2,1,0:T(8,128)(2,1)}) %all-gather.11.cloned.1.call-update) | async-done | bytes 9437200 | tf_op jit(solution)/shard_map/all_gather | solution.py:268
  108.8 5.2 fusion.8
  126.8 40.8 %all-gather.13.cloned.1.call-done = bf16[1,1536,1536]{2,1,0:T(8,128)(2,1)} async-done(((bf16[1,384,1536]{2,1,0:T(8,128)(2,1)}), bf16[1,1536,1536]{2,1,0:T(8,128)(2,1)}) %all-gather.13.cloned.1.call-update) | async-done | bytes 4718608 | tf_op jit(solution)/shard_map/all_gather | solution.py:269
  167.6 3.8 multiply_reduce_fusion.2
  171.5 225.6 %all-gather.15.cloned.1.call-done = bf16[1,1536,8192]{2,1,0:T(8,128)(2,1)} async-done(((bf16[1,384,8192]{2,1,0:T(8,128)(2,1)}), bf16[1,1536,8192]{2,1,0:T(8,128)(2,1)}) %all-gather.15.cloned.1.call-update) | async-done | bytes 25165840 | tf_op jit(solution)/shard_map/all_gather | solution.py:276
  397.1 13.8 fusion.2
  410.9 110.3 %all-gather.17.cloned.1.call-done = bf16[1,4096,1536]{2,1,0:T(8,128)(2,1)} async-done(((bf16[1,1024,1536]{2,1,0:T(8,128)(2,1)}), bf16[1,4096,1536]{2,1,0:T(8,128)(2,1)}) %all-gather.17.cloned.1.call-update) | async-done | bytes 12582928 | tf_op jit(solution)/shard_map/all_gather | solution.py:288
  521.2 10.4 multiply_convert_fusion.1
  531.6 14.9 %multiply_reduce_fusion = (bf16[1536]{0:T(1024)(128)(2,1)}, f32[256]{0:T(256)S(1)}, f32[256,1536]{1,0:T(8,128)}) fusion(f32[256,1536]{1,0:T(8,128)S(1)} %get-tuple-element.44, f32[256]{0:T(256)S(1)} %add_rsqrt_fusion, f32[1536]{0:T(1024)S(1)} %convert_reduce_fusion, bf16[1,1536,8192]{2,1,0:T(8,128)(2,1)} %all-gather.15.cloned.1.call-done, ...), kind=kOutput, calls=%fused_computation.61 | convolution fusion | flops 6453196800 | bytes 32517120 | tf_op jit(solution)/shard_map/dot_general | solution.py:83
  548.5 3.6 convolution_convert_fusion.3
  552.2 4.6 fusion.24
  559.1 4.2 fusion.14
  570.3 7.3 convolution_convert_fusion.2
  577.6 10.3 convolution_convert_fusion.1
  588.0 14.2 convolution_convert_fusion
  605.2 5.5 reduce-scatter.7.cloned.1.call-done
  610.7 174.9 %reduce-scatter.5.cloned.1.call-done = bf16[384,3072]{1,0:T(8,128)(2,1)} async-done(((bf16[1536,3072]{1,0:T(8,128)(2,1)}), bf16[384,3072]{1,0:T(8,128)(2,1)}) %reduce-scatter.5.cloned.1.call-update) | async-done | bytes 2359312 | tf_op jit(solution)/shard_map/reduce_scatter | solution.py:324
  785.6 155.7 %reduce-scatter.11.cloned.1.call-done = bf16[1024,1536]{1,0:T(8,128)(2,1)} async-done(((bf16[4096,1536]{1,0:T(8,128)(2,1)}), bf16[1024,1536]{1,0:T(8,128)(2,1)}) %reduce-scatter.11.cloned.1.call-update) | async-done | bytes 3145744 | tf_op jit(solution)/shard_map/reduce_scatter | solution.py:300
  941.3 224.8 %reduce-scatter.9.cloned.1.call-done = bf16[384,8192]{1,0:T(8,128)(2,1)} async-done(((bf16[1536,8192]{1,0:T(8,128)(2,1)}), bf16[384,8192]{1,0:T(8,128)(2,1)}) %reduce-scatter.9.cloned.1.call-update) | async-done | bytes 6291472 | tf_op jit(solution)/shard_map/reduce_scatter | solution.py:297
  1169.2 6.1 broadcast_in_dim.35
  1177.2 4.4 constant_dynamic-update-slice_fusion.2
  1181.6 4.0 constant_dynamic-update-slice_fusion.1
  1185.6 51.8 %collective-permute-done.2 = bf16[1024,1536]{1,0:T(8,128)(2,1)} collective-permute-done((bf16[1024,1536]{1,0:T(8,128)(2,1)}, bf16[1024,1536]{1,0:T(8,128)(2,1)}, u32[]{:S(2)}, u32[]{:S(2)}) %collective-permute-start.2) | collective-permute-done | bytes 3145760 | tf_op jit(solution)/shard_map/ppermute | solution.py:25
  1237.4 3.8 constant_dynamic-update-slice_fusion
  1241.2 4.7 fusion.37
  1245.9 8.4 all-reduce.4
  1254.5 14.5 all-reduce.2
  1274.0 9.0 fusion.23
  1283.0 148.2 %all-reduce.7.cloned.1.call-done = (bf16[1,384,3072]{2,1,0:T(8,128)(2,1)}, bf16[1,384,1536]{2,1,0:T(8,128)(2,1)}, bf16[1,384,8192]{2,1,0:T(8,128)(2,1)}, bf16[1,1024,1536]{2,1,0:T(8,128)(2,1)}) async-done(((bf16[1,384,3072]{2,1,0:T(8,128)(2,1)}, bf16[1,384,1536]{2,1,0:T(8,128)(2,1)}, bf16[1,384,8192]{2,1,0:T(8,128)(2,1)}, bf16[1,1024,1536]{2,1,0:T(8,128)(2,1)}), (bf16[1,384,3072]{2,1,0:T(8,128)(2,1)}, ...) | async-done | bytes 12976144 | tf_op jit(solution)/shard_map/psum | solution.py:235
  1431.2 9.3 stack.45
  (174 shorter events, 50.2 us)
Async XLA Ops:
  7.2 101.6 %all-gather.11.cloned.1.call-start = ((), (), s32[]{:S(2)}) async-start(), calls=%async_computation.8 | async-start | bytes 11796480 | tf_op jit(solution)/shard_map/all_gather | solution.py:268
  7.9 159.7 %all-gather.13.cloned.1.call-start = ((), (), s32[]{:S(2)}) async-start(), calls=%async_computation.9 | async-start | bytes 5898240 | tf_op jit(solution)/shard_map/all_gather | solution.py:269
  8.7 388.4 %all-gather.15.cloned.1.call-start = ((), (), s32[]{:S(2)}) async-start(), calls=%async_computation.10 | async-start | bytes 31457280 | tf_op jit(solution)/shard_map/all_gather | solution.py:276
  9.4 18.5 %copy-start.43 = (s32[64]{0:T(128)S(1)}, s32[64]{0:T(128)}, u32[]{:S(2)}) copy-start(s32[64]{0:T(128)} %param.14) | copy-start | bytes 772
  9.4 18.6 %copy-start.41 = (s32[64]{0:T(128)S(1)}, s32[64]{0:T(128)}, u32[]{:S(2)}) copy-start(s32[64]{0:T(128)} %param.15) | copy-start | bytes 772
  9.4 18.6 %copy-start.42 = (s32[64]{0:T(128)S(1)}, s32[64]{0:T(128)}, u32[]{:S(2)}) copy-start(s32[64]{0:T(128)} %param.13) | copy-start | bytes 772
  9.4 19.7 %copy-start.2 = (bf16[256,1536]{1,0:T(8,128)(2,1)S(1)}, bf16[256,1536]{1,0:T(8,128)(2,1)}, u32[]{:S(2)}) copy-start(bf16[256,1536]{1,0:T(8,128)(2,1)} %param.11) | copy-start | bytes 2359300
  9.4 511.8 %all-gather.17.cloned.1.call-start = ((), (), s32[]{:S(2)}) async-start(), calls=%async_computation.11 | async-start | bytes 15728640 | tf_op jit(solution)/shard_map/all_gather | solution.py:288
  10.0 600.7 %reduce-scatter.7.cloned.1.call-start = ((), (), s32[]{:S(2)}) async-start(), calls=%async_computation.5 | async-start | bytes 5898240 | tf_op jit(solution)/shard_map/reduce_scatter | solution.py:327
  29.4 84.6 %copy-start.33 = (f32[256]{0:T(256)}, f32[256]{0:T(256)S(1)}, u32[]{:S(2)}) copy-start(f32[256]{0:T(256)S(1)} %add_rsqrt_fusion.1) | copy-start | bytes 3076
  124.6 43.0 %copy-start.30 = (f32[2,8,256]{2,1,0:T(8,128)}, f32[2,8,256]{2,1,0:T(8,128)S(1)}, u32[]{:S(2)}) copy-start(f32[2,8,256]{2,1,0:T(8,128)S(1)} %log_add_fusion) | copy-start | bytes 49156
  126.8 44.6 %copy-start.6 = (bf16[8,96,2,256]{3,1,2,0:T(8,128)(2,1)}, bf16[8,96,2,256]{3,1,2,0:T(8,128)(2,1)S(1)}, u32[]{:S(2)}) copy-start(bf16[8,96,2,256]{3,1,2,0:T(8,128)(2,1)S(1)} %convolution_convert_fusion.4) | copy-start | bytes 2359300
  171.4 360.2 %copy-start.32 = (f32[256]{0:T(256)}, f32[256]{0:T(256)S(1)}, u32[]{:S(2)}) copy-start(f32[256]{0:T(256)S(1)} %add_rsqrt_fusion) | copy-start | bytes 3076
  397.1 124.1 %copy-start.11 = (bf16[256,1536]{1,0:T(8,128)(2,1)S(1)}, bf16[256,1536]{1,0:T(8,128)(2,1)}, u32[]{:S(2)}) copy-start(bf16[256,1536]{1,0:T(8,128)(2,1)} %param.12) | copy-start | bytes 2359300
  397.1 124.2 %copy-start.36 = (f32[256]{0:T(256)S(1)}, f32[256]{0:T(256)}, u32[]{:S(2)}) copy-start(f32[256]{0:T(256)} %compare_convert_fusion) | copy-start | bytes 3076
  531.6 14.9 %copy-start.12 = (bf16[256,1536]{1,0:T(8,128)(2,1)S(1)}, bf16[256,1536]{1,0:T(8,128)(2,1)}, u32[]{:S(2)}) copy-start(bf16[256,1536]{1,0:T(8,128)(2,1)} %param.12) | copy-start | bytes 2359300
  531.6 14.9 %copy-start.37 = (f32[256]{0:T(256)S(1)}, f32[256]{0:T(256)}, u32[]{:S(2)}) copy-start(f32[256]{0:T(256)} %compare_convert_fusion) | copy-start | bytes 3076
  552.1 233.5 %reduce-scatter.5.cloned.1.call-start = ((), (), s32[]{:S(2)}) async-start(), calls=%async_computation.4 | async-start | bytes 11796480 | tf_op jit(solution)/shard_map/reduce_scatter | solution.py:324
  577.6 363.8 %reduce-scatter.11.cloned.1.call-start = ((), (), s32[]{:S(2)}) async-start(), calls=%async_computation.7 | async-start | bytes 15728640 | tf_op jit(solution)/shard_map/reduce_scatter | solution.py:300
  587.9 578.3 %reduce-scatter.9.cloned.1.call-start = ((), (), s32[]{:S(2)}) async-start(), calls=%async_computation.6 | async-start | bytes 31457280 | tf_op jit(solution)/shard_map/reduce_scatter | solution.py:297
  602.2 829.0 %all-reduce.7.cloned.1.call-start = ((), (), s32[]{:S(2)}) async-start(), calls=%async_computation.12 | async-start | bytes 25952256 | tf_op jit(solution)/shard_map/psum | solution.py:235
  602.2 564.0 %collective-permute-start = (bf16[1024,1536]{1,0:T(8,128)(2,1)}, bf16[1024,1536]{1,0:T(8,128)(2,1)}, u32[]{:S(2)}, u32[]{:S(2)}) collective-permute-start(bf16[1024,1536]{1,0:T(8,128)(2,1)} %bitcast.127), channel_id=1, source_target_pairs={{0,8},{8,16},{16,24},{24,0},{1,9},{9,17},{17,25},{25,1},{2,10},{10... | collective-permute-start | bytes 9437192 | tf_op jit(solution)/shard_map/ppermute | solution.py:25
  603.8 577.8 %collective-permute-start.1 = (bf16[1024,1536]{1,0:T(8,128)(2,1)}, bf16[1024,1536]{1,0:T(8,128)(2,1)}, u32[]{:S(2)}, u32[]{:S(2)}) collective-permute-start(bf16[1024,1536]{1,0:T(8,128)(2,1)} %bitcast.128), channel_id=1, source_target_pairs={{0,24},{8,0},{16,8},{24,16},{1,25},{9,1},{17,9},{25,17},{2,26},{10... | collective-permute-start | bytes 9437192 | tf_op jit(solution)/shard_map/ppermute | solution.py:30
  1166.2 71.2 %collective-permute-start.2 = (bf16[1024,1536]{1,0:T(8,128)(2,1)}, bf16[1024,1536]{1,0:T(8,128)(2,1)}, u32[]{:S(2)}, u32[]{:S(2)}) collective-permute-start(bf16[1024,1536]{1,0:T(8,128)(2,1)} %collective-permute-done), channel_id=1, source_target_pairs={{0,8},{8,16},{16,24},{24,0},{1,9},{9,17},{17,25},{25,1},{2,10},{10... | collective-permute-start | bytes 9437192 | tf_op jit(solution)/shard_map/ppermute | solution.py:25
  1175.3 65.8 %slice-start = ((s8[9437184]{0:T(1024)(128)(4,1)}), s8[4194304]{0:T(1024)(128)(4,1)S(1)}, s32[]{:S(2)}) async-start(s8[9437184]{0:T(1024)(128)(4,1)} %bitcast.153), calls=%async_computation.13 | async-start | bytes 8388608
  1177.2 63.9 %slice-start.1 = ((s8[9437184]{0:T(1024)(128)(4,1)}), s8[4194304]{0:T(1024)(128)(4,1)S(1)}, s32[]{:S(2)}) async-start(s8[9437184]{0:T(1024)(128)(4,1)} %bitcast.153), calls=%async_computation.14 | async-start | bytes 8388608
  1181.6 59.5 %slice-start.2 = ((s8[9437184]{0:T(1024)(128)(4,1)}), s8[1048576]{0:T(1024)(128)(4,1)S(1)}, s32[]{:S(2)}) async-start(s8[9437184]{0:T(1024)(128)(4,1)} %bitcast.153), calls=%async_computation.15 | async-start | bytes 2097152
  1185.6 55.5 %copy-start.4 = (bf16[256,1536]{1,0:T(8,128)(2,1)S(1)}, bf16[256,1536]{1,0:T(8,128)(2,1)}, u32[]{:S(2)}) copy-start(bf16[256,1536]{1,0:T(8,128)(2,1)} %param.11) | copy-start | bytes 2359300
  1185.6 55.5 %copy-start.16 = (bf16[256,1536]{0,1:T(8,128)(2,1)S(1)}, bf16[256,1536]{0,1:T(8,128)(2,1)}, u32[]{:S(2)}) copy-start(bf16[256,1536]{0,1:T(8,128)(2,1)} %copy-done.15) | copy-start | bytes 2359300
  1185.6 55.5 %copy-start.29 = (bf16[8,96,256]{2,1,0:T(8,128)(2,1)S(1)}, bf16[8,96,256]{2,1,0:T(8,128)(2,1)}, u32[]{:S(2)}) copy-start(bf16[8,96,256]{2,1,0:T(8,128)(2,1)} %copy-done.28) | copy-start | bytes 1179652
  1185.6 55.6 %copy-start.35 = (f32[256]{0:T(256)S(1)}, f32[256]{0:T(256)}, u32[]{:S(2)}) copy-start(f32[256]{0:T(256)} %copy-done.33) | copy-start | bytes 3076
  1245.9 28.2 %copy-start.38 = (f32[256]{0:T(256)S(1)}, f32[256]{0:T(256)}, u32[]{:S(2)}) copy-start(f32[256]{0:T(256)} %compare_convert_fusion) | copy-start | bytes 3076
  (28 other events, 104.8 us)
Sparse Core Ops, SparseCore 0:
  9.8 98.9 all-gather.10
  110.6 56.9 all-gather.12
  169.5 227.5 all-gather.14
  398.8 122.4 all-gather.16
  552.2 58.4 reduce-scatter.6
  613.7 171.8 reduce-scatter.4
  789.3 152.0 reduce-scatter.10
  944.4 221.6 reduce-scatter.8
  1168.8 262.3 all-reduce.6
